TPU v7x, 32 devices: a whole 2x2x4 slice. The times are simulated.
32 devices in a mesh: member: 4 (over y, x), grid: 8 (over z, core).
Axes of the slice: x: 2, y: 2, z: 4, core: 2. Of those that a mesh axis runs over, the one named last changes fastest.
Arguments:
- prior_ensemble: bfloat16 [40, 48, 32768], P('member', None, 'grid'), may hold values from -6 to 6
- domain_site_mapping: int32 [8, 4, 1024], P(None, None, 'grid'), may hold values from 0 to 4095, as said below
- neighbour_triples: int32 [8, 3, 4096], P('grid', None, 'member'), may hold values from 0 to 159
- stencil_factors: float32 [8, 3, 4096], P('grid', None, 'member'), may hold values from 0.1 to 1
- sparse_node_transforms: float32 [1600, 1024], P(None, 'grid'), may hold values from -0.4 to 1.8
Outputs:
- analysis: bfloat16 [40, 48, 32768], P('member', None, 'grid')
Inputs may be any that keep to these rules, and one draw needn't show every extreme that they name: For every model patch h, the entries domain_site_mapping[:, :, h * 128 : (h + 1) * 128] hold every number from 0 to 4095 exactly once.
All inputs are finite; a program needn't handle non-finite values.
Results may differ from a plain program's by a relative error of at most 0.0076.
Values may be sent and summed in bfloat16 or wider, within the bound.
A program may use at most 128 MiB of HBM per device.

v0:
```python
import functools

import jax
import jax.numpy as jnp
from jax import lax
from jax.experimental import pallas as pl
from jax.experimental.pallas import tpu as pltpu
from jax.sharding import PartitionSpec as P

RIM = 16
DIGIT = 128
CHUNKS = 2


def update_kernel(ids_ref, share_ref, t_ref, x_ref, out_ref, w_ref, dev_ref, mean_ref, acc_ref):
    members, fields, width = x_ref.shape
    pairs, coarse = t_ref.shape
    slots = lax.broadcasted_iota(jnp.int32, (coarse, width), 0)
    spread = jnp.zeros((coarse, width), jnp.float32)
    for s in range(3):
        spread = spread + jnp.where(ids_ref[s : s + 1, :] == slots, share_ref[s : s + 1, :], 0.0)
    spread = spread.astype(jnp.bfloat16)
    rows = pairs // 10

    def blend(i, carry):
        at = pl.ds(pl.multiple_of(i * rows, rows), rows)
        part = jnp.dot(t_ref[at, :], spread, preferred_element_type=jnp.float32)
        w_ref[pl.ds(i * (rows // 8), rows // 8)] = part.reshape(rows // 8, 8, width)
        return carry

    lax.fori_loop(0, 10, blend, 0)

    def add(k, total):
        return total + x_ref[k].astype(jnp.float32)

    mean_ref[...] = (
        lax.fori_loop(0, members, add, jnp.zeros((fields, width), jnp.float32)) / members
    )

    def center(k, carry):
        d = x_ref[k].astype(jnp.float32) - mean_ref[...]
        dev_ref[k] = d.astype(jnp.bfloat16).astype(jnp.float32)
        return carry

    lax.fori_loop(0, members, center, 0)
    group = 8
    unroll = 8
    half = fields // 2
    for lane in range(0, width, 128):
        lanes = slice(lane, lane + 128)
        for field in (0, half):
            some_fields = slice(field, field + half)

            def contract(jg, carry, lanes=lanes, some_fields=some_fields):
                def some(kk, accs):
                    accs = list(accs)
                    for u in range(unroll):
                        k = kk * unroll + u
                        d = dev_ref[k, some_fields, lanes]
                        for jj in range(group):
                            w = w_ref[k * (members // group) + jg, jj : jj + 1, lanes]
                            accs[jj] = accs[jj] + d * w
                    return tuple(accs)

                first = tuple(mean_ref[some_fields, lanes] for _ in range(group))
                accs = lax.fori_loop(0, members // unroll, some, first)
                for jj in range(group):
                    acc_ref[jg * group + jj, some_fields, lanes] = accs[jj]
                return carry

            lax.fori_loop(0, members // group, contract, 0)
    lax.fori_loop(0, members, lambda j, c: store(j, c, out_ref, acc_ref), 0)


def store(j, carry, out_ref, acc_ref):
    out_ref[j] = acc_ref[j].astype(jnp.bfloat16)
    return carry


def update(ids, shares, transforms, gathered):
    members, fields, columns = gathered.shape
    pairs, coarse = transforms.shape
    width = min(256, columns)
    flops = 2 * pairs * columns * (coarse + 8 * fields)
    return pl.pallas_call(
        update_kernel,
        grid=(columns // width,),
        out_shape=jax.ShapeDtypeStruct(gathered.shape, jnp.bfloat16),
        in_specs=[
            pl.BlockSpec((3, width), lambda i: (0, i)),
            pl.BlockSpec((3, width), lambda i: (0, i)),
            pl.BlockSpec((pairs, coarse), lambda i: (0, 0)),
            pl.BlockSpec((members, fields, width), lambda i: (0, 0, i)),
        ],
        out_specs=pl.BlockSpec((members, fields, width), lambda i: (0, 0, i)),
        scratch_shapes=[
            pltpu.VMEM((pairs // 8, 8, width), jnp.float32),
            pltpu.VMEM((members, fields, width), jnp.float32),
            pltpu.VMEM((fields, width), jnp.float32),
            pltpu.VMEM((members, fields, width), jnp.float32),
        ],
        compiler_params=pltpu.CompilerParams(vmem_limit_bytes=62 * 1024 * 1024),
        cost_estimate=pl.CostEstimate(flops=flops, bytes_accessed=12_000_000, transcendentals=0),
    )(ids, shares, transforms, gathered)


def assemble_kernel(*refs):
    out_ref = refs[-1]
    part = refs[0].shape[3]

    def put(k, carry):
        for i, ref in enumerate(refs[:-1]):
            out_ref[k, :, i * part : (i + 1) * part] = ref[0, k]
        return carry

    lax.fori_loop(0, out_ref.shape[0], put, 0)


def assemble(results):
    groups, members, fields, part = results[0].shape
    width = part * len(results)
    return pl.pallas_call(
        assemble_kernel,
        grid=(groups,),
        out_shape=jax.ShapeDtypeStruct((members, fields, groups * width), results[0].dtype),
        in_specs=[pl.BlockSpec((1, members, fields, part), lambda i: (i, 0, 0, 0))] * len(results),
        out_specs=pl.BlockSpec((members, fields, width), lambda i: (0, 0, i)),
    )(*results)


def on_device(prior, mapping, triples, factors, transforms):
    groups = lax.axis_size("member")
    patches = lax.axis_size("grid")
    cells = prior.shape[2]
    columns = cells // groups
    per_source = columns // patches
    coarse_dev = transforms.shape[1]
    coarse = coarse_dev * patches

    everywhere = lax.all_gather(transforms.astype(jnp.bfloat16), "grid", axis=1, tiled=True)

    region = lax.axis_index("grid")
    ids = (region * coarse_dev - RIM + triples[0] + coarse) % coarse
    raw = factors[0]
    shares = raw / jnp.sum(raw, axis=0, keepdims=True)
    table = jnp.concatenate(
        [
            (ids // DIGIT).astype(jnp.bfloat16),
            (ids % DIGIT).astype(jnp.bfloat16),
            shares.astype(jnp.bfloat16),
        ],
        axis=0,
    )
    table = jnp.transpose(table.reshape(9, patches, per_source), (1, 0, 2))
    table = jnp.broadcast_to(table[None], (groups, patches, 9, per_source))
    table = table.reshape(groups * patches, 9, per_source)
    part = columns // CHUNKS
    exchanged = []
    for chunk in range(CHUNKS):
        starts = [m * columns + chunk * part for m in range(groups)]
        blocks = jnp.stack([prior[:, :, at : at + part] for at in starts])
        exchanged.append(
            lax.all_to_all(blocks, "member", split_axis=0, concat_axis=0, tiled=True)
        )
    table = lax.all_to_all(table, ("member", "grid"), split_axis=0, concat_axis=0, tiled=True)
    table = jnp.transpose(table, (1, 0, 2)).reshape(9, cells)
    spots = jnp.transpose(mapping, (1, 0, 2)).reshape(cells)
    mine = lax.axis_index("member") * columns + jnp.arange(columns, dtype=jnp.int32)
    onehot = (spots[:, None] == mine[None, :]).astype(jnp.bfloat16)
    found = jnp.dot(table, onehot, preferred_element_type=jnp.float32)
    cell_ids = (found[0:3] * DIGIT + found[3:6]).astype(jnp.int32)
    cell_shares = found[6:9]

    results = []
    for chunk in range(CHUNKS):
        here = slice(chunk * part, (chunk + 1) * part)
        blocks = exchanged[chunk]
        gathered = blocks.reshape((-1,) + blocks.shape[2:])
        result = update(cell_ids[:, here], cell_shares[:, here], everywhere, gathered)
        result = result.reshape(blocks.shape)
        results.append(
            lax.all_to_all(result, "member", split_axis=0, concat_axis=0, tiled=True)
        )
    return assemble(results)


def solution(mesh):
    return jax.shard_map(
        on_device,
        mesh=mesh,
        in_specs=(
            P("member", None, "grid"),
            P(None, None, "grid"),
            P("grid", None, "member"),
            P("grid", None, "member"),
            P(None, "grid"),
        ),
        out_specs=P("member", None, "grid"),
        check_vma=False,
    )
```

profile of v0, /device:TPU:0, one launch (start us, length us, event | category | flops | bytes accessed | tf_op | source)
XLA Modules:
  0.0 161.8 jit_solution(7375596572523650484)
XLA Ops:
  6.5 0.0 all-gather.2.cloned.1.call-start
  6.5 1.9 %convert_element_type.23 = bf16[1600,128]{1,0:T(8,128)(2,1)} convert(f32[1600,128]{1,0:T(8,128)} %param.9) | non-fusion elementwise | flops 204800 | bytes 1228800 | tf_op jit(solution)/shard_map/convert_element_type | solution.py:140
  8.5 0.0 all-gather.2.cloned.1.call-update
  8.5 0.7 reduce_sum.9
  9.2 0.7 divide_convert_fusion
  9.9 0.7 add_add_fusion
  10.7 0.7 broadcast_in_dim.2
  11.4 7.3 %all-to-all-start = ((bf16[32,9,128]{2,1,0:T(8,128)(2,1)}), bf16[32,9,128]{2,1,0:T(8,128)(2,1)S(1)}, u32[]{:S(2)}, u32[]{:S(2)}) async-start(bf16[32,9,128]{2,1,0:T(8,128)(2,1)} %bitcast.4), calls=%async_computation | async-start | bytes 262144 | tf_op jit(solution)/shard_map/all_to_all | solution.py:165
  18.7 3.6 %slice_bitcast_fusion.3 = (bf16[1,10,48,512]{3,2,1,0:T(8,128)(2,1)S(1)}, bf16[1,10,48,512]{3,2,1,0:T(8,128)(2,1)S(1)}, bf16[1,10,48,512]{3,2,1,0:T(8,128)(2,1)S(...) fusion(bf16[10,48,4096]{2,1,0:T(8,128)(2,1)} %param.5), kind=kLoop, calls=%fused_computation.9 | loop fusion | bytes 7864320 | tf_op jit(solution)/shard_map/stack | solution.py:161
  22.3 1.6 pad_maximum_fusion.1
  23.9 7.1 %all-to-all-done = bf16[32,9,128]{2,1,0:T(8,128)(2,1)S(1)} async-done(((bf16[32,9,128]{2,1,0:T(8,128)(2,1)}), bf16[32,9,128]{2,1,0:T(8,128)(2,1)S(1)}, u32[]{:S(2)}, u32[]{:S(2)}) %all-to-all-start) | async-done | bytes 73760 | tf_op jit(solution)/shard_map/all_to_all | solution.py:165
  30.9 0.7 copy-done.3
  31.6 3.6 %all-to-all-start.3 = ((bf16[4,10,48,512]{3,2,1,0:T(8,128)(2,1)}), bf16[4,10,48,512]{3,2,1,0:T(8,128)(2,1)S(1)}, u32[]{:S(2)}, u32[]{:S(2)}) async-start(bf16[4,10,48,512]{3,2,1,0:T(8,128)(2,1)} %pad_maximum_fusion.1), calls=%async_computation.3 | async-start | bytes 3932160 | tf_op jit(solution)/shard_map/all_to_all | solution.py:163
  35.2 2.6 %pad_maximum_fusion = bf16[4,10,48,512]{3,2,1,0:T(8,128)(2,1)} fusion(bf16[1,10,48,512]{3,2,1,0:T(8,128)(2,1)S(1)} %get-tuple-element.7, bf16[1,10,48,512]{3,2,1,0:T(8,128)(2,1)S(1)} %get-tuple-element.8, bf16[1,10,48,512]{3,2,1,0:T(8,128)(2,1)S(1)} %get-tuple-element.9, bf16[1,10,48,512]{3,2,1,0:T(8,128)(2,1)} %get-tuple-element.10), kind=kLoop, calls=%fused_computation.4 | loop fusion | flops 2949120 | bytes 3932160 | tf_op jit(solution)/shard_map/stack | solution.py:161
  37.7 21.9 %all-to-all-done.3 = bf16[4,10,48,512]{3,2,1,0:T(8,128)(2,1)S(1)} async-done(((bf16[4,10,48,512]{3,2,1,0:T(8,128)(2,1)}), bf16[4,10,48,512]{3,2,1,0:T(8,128)(2,1)S(1)}, u32[]{:S(2)}, u32[]{:S(2)}) %all-to-all-start.3) | async-done | bytes 1966112 | tf_op jit(solution)/shard_map/all_to_all | solution.py:163
  59.7 1.3 copy-done.2
  61.0 3.6 %all-to-all-start.1 = ((bf16[4,10,48,512]{3,2,1,0:T(8,128)(2,1)}), bf16[4,10,48,512]{3,2,1,0:T(8,128)(2,1)S(1)}, u32[]{:S(2)}, u32[]{:S(2)}) async-start(bf16[4,10,48,512]{3,2,1,0:T(8,128)(2,1)} %pad_maximum_fusion), calls=%async_computation.1 | async-start | bytes 3932160 | tf_op jit(solution)/shard_map/all_to_all | solution.py:163
  64.6 0.0 copy-done.5
  64.6 0.0 copy-done.4
  64.7 0.1 copy.11
  64.8 2.6 %fusion = f32[9,1024]{1,0:T(8,128)S(1)} fusion(bf16[9,4096]{1,0:T(8,128)(2,1)S(1)} %bitcast.42, s32[1024]{0:T(1024)S(1)} %iota_add_fusion, s32[4096]{0:T(1024)S(1)} %bitcast.45), kind=kOutput, calls=%fused_computation | convolution fusion | flops 79691776 | bytes 131072 | tf_op jit(solution)/shard_map/dot_general | solution.py:170
  67.4 0.6 fusion.11
  68.0 0.6 fusion.10
  68.6 23.9 %shard_map.56 = bf16[40,48,512]{2,1,0:T(8,128)(2,1)} custom-call(s32[3,512]{1,0:T(4,128)} %get-tuple-element.15.ids_ref, f32[3,512]{1,0:T(4,128)} %get-tuple-element.13.share_ref, bf16[1600,1024]{1,0:T(8,128)(2,1)} %all-gather.2.cloned.1.call-done.t_ref, bf16[40,48,512]{2,1,0:T(8,128)(2,1)} %bitcast.37), custom_call_target="tpu_custom_call" | custom-call | flops 2306867200 | bytes 12000000 | tf_op jit(solution)/shard_map/pallas_call | solution.py:85
  92.5 0.0 all-to-all-done.1
  92.5 1.3 copy-done.1
  93.8 4.1 %all-to-all-start.4 = ((bf16[4,10,48,512]{3,2,1,0:T(8,128)(2,1)}), bf16[4,10,48,512]{3,2,1,0:T(8,128)(2,1)S(1)}, u32[]{:S(2)}, u32[]{:S(2)}) async-start(bf16[4,10,48,512]{3,2,1,0:T(8,128)(2,1)} %bitcast.38), calls=%async_computation.4 | async-start | bytes 3932160 | tf_op jit(solution)/shard_map/all_to_all | solution.py:182
  97.9 23.9 %shard_map.55 = bf16[40,48,512]{2,1,0:T(8,128)(2,1)} custom-call(s32[3,512]{1,0:T(4,128)} %get-tuple-element.16.ids_ref, f32[3,512]{1,0:T(4,128)} %get-tuple-element.14.share_ref, bf16[1600,1024]{1,0:T(8,128)(2,1)} %all-gather.2.cloned.1.call-done.t_ref, bf16[40,48,512]{2,1,0:T(8,128)(2,1)} %bitcast.36), custom_call_target="tpu_custom_call" | custom-call | flops 2306867200 | bytes 12000000 | tf_op jit(solution)/shard_map/pallas_call | solution.py:85
  121.9 0.0 all-to-all-done.4.refs_1_
  121.9 28.5 %all_to_all.25.refs_0_ = bf16[4,10,48,512]{3,2,1,0:T(8,128)(2,1)} all-to-all(bf16[4,10,48,512]{3,2,1,0:T(8,128)(2,1)} %bitcast.39), channel_id=1, replica_groups=mesh['member'=4,'grid'=8] {'member'}, dimensions={0} | all-to-all | bytes 3932160 | tf_op jit(solution)/shard_map/all_to_all | solution.py:182
  150.4 0.0 copy-done
  150.4 4.6 %shard_map.57 = bf16[10,48,4096]{2,1,0:T(8,128)(2,1)} custom-call(bf16[4,10,48,512]{3,2,1,0:T(8,128)(2,1)} %all_to_all.25.refs_0_, bf16[4,10,48,512]{3,2,1,0:T(8,128)(2,1)} %copy-done), custom_call_target="tpu_custom_call" | custom-call | tf_op jit(solution)/shard_map/pallas_call | solution.py:122
  (15 shorter events, 0.1 us)
Async XLA Ops:
  6.5 62.1 %all-gather.2.cloned.1.call-start = ((), (), s32[]{:S(2)}) async-start(), calls=%async_computation.5 | async-start | bytes 3686400 | tf_op jit(solution)/shard_map/all_gather | solution.py:140
  11.4 19.5 %all-to-all-start = ((bf16[32,9,128]{2,1,0:T(8,128)(2,1)}), bf16[32,9,128]{2,1,0:T(8,128)(2,1)S(1)}, u32[]{:S(2)}, u32[]{:S(2)}) async-start(bf16[32,9,128]{2,1,0:T(8,128)(2,1)} %bitcast.4), calls=%async_computation | async-start | bytes 262144 | tf_op jit(solution)/shard_map/all_to_all | solution.py:165
  30.9 0.7 copy-start.3
  31.6 28.1 %all-to-all-start.3 = ((bf16[4,10,48,512]{3,2,1,0:T(8,128)(2,1)}), bf16[4,10,48,512]{3,2,1,0:T(8,128)(2,1)S(1)}, u32[]{:S(2)}, u32[]{:S(2)}) async-start(bf16[4,10,48,512]{3,2,1,0:T(8,128)(2,1)} %pad_maximum_fusion.1), calls=%async_computation.3 | async-start | bytes 3932160 | tf_op jit(solution)/shard_map/all_to_all | solution.py:163
  37.7 26.9 %copy-start.5 = (s32[8,4,128]{2,1,0:T(4,128)S(1)}, s32[8,4,128]{2,1,0:T(4,128)}, u32[]{:S(2)}) copy-start(s32[8,4,128]{2,1,0:T(4,128)} %param.6) | copy-start | bytes 49156
  37.7 26.9 %copy-start.4 = (bf16[32,9,128]{2,1,0:T(8,128)(2,1)S(1)}, bf16[32,9,128]{2,1,0:T(8,128)(2,1)}, u32[]{:S(2)}) copy-start(bf16[32,9,128]{2,1,0:T(8,128)(2,1)} %copy-done.3) | copy-start | bytes 221188
  59.7 1.3 copy-start.2
  61.0 31.5 %all-to-all-start.1 = ((bf16[4,10,48,512]{3,2,1,0:T(8,128)(2,1)}), bf16[4,10,48,512]{3,2,1,0:T(8,128)(2,1)S(1)}, u32[]{:S(2)}, u32[]{:S(2)}) async-start(bf16[4,10,48,512]{3,2,1,0:T(8,128)(2,1)} %pad_maximum_fusion), calls=%async_computation.1 | async-start | bytes 3932160 | tf_op jit(solution)/shard_map/all_to_all | solution.py:163
  92.5 1.3 copy-start.1
  93.8 28.1 %all-to-all-start.4 = ((bf16[4,10,48,512]{3,2,1,0:T(8,128)(2,1)}), bf16[4,10,48,512]{3,2,1,0:T(8,128)(2,1)S(1)}, u32[]{:S(2)}, u32[]{:S(2)}) async-start(bf16[4,10,48,512]{3,2,1,0:T(8,128)(2,1)} %bitcast.38), calls=%async_computation.4 | async-start | bytes 3932160 | tf_op jit(solution)/shard_map/all_to_all | solution.py:182
  121.9 28.5 %copy-start = (bf16[4,10,48,512]{3,2,1,0:T(8,128)(2,1)}, bf16[4,10,48,512]{3,2,1,0:T(8,128)(2,1)S(1)}, u32[]{:S(2)}) copy-start(bf16[4,10,48,512]{3,2,1,0:T(8,128)(2,1)S(1)} %all-to-all-done.4.refs_1_) | copy-start | bytes 5898244
Sparse Core Ops, SparseCore 0:
  8.9 46.8 all-gather.1
where the time goes:
time: 163 us; the launch traced here: 162 us
  Pallas kernels  52.4 us (32%)
  waiting for transfers between devices  29 us (18%)
  blocking collectives  28.5 us (17%)
  starting transfers between devices  18.7 us (11%)
  between operations  13.5 us (8%)
  local copies, waits for them, and re-layouts  8.79 us (5%)
  other arithmetic  8.24 us (5%)
  matrix products  2.61 us (2%)
    pallas_call x2, Pallas kernels, update(): pl.pallas_call(update_kernel, grid=(columns // width,), out_shape=jax.Sha...  47.9 us
    all_to_all x1, blocking collectives, on_device(): lax.all_to_all(result, 'member', split_axis=0, concat_axis=0, tiled=True)  28.5 us
    all_to_all x2, waiting for transfers between devices, on_device(): lax.all_to_all(blocks, 'member', split_axis=0, concat_axis=0, tiled=True)  22 us
    all_to_all x1, starting transfers between devices, on_device(): lax.all_to_all(table, ('member', 'grid'), split_axis=0, concat_axis=0, ti...  7.33 us
    all_to_all x2, starting transfers between devices, on_device(): lax.all_to_all(blocks, 'member', split_axis=0, concat_axis=0, tiled=True)  7.19 us
    all_to_all x1, waiting for transfers between devices, on_device(): lax.all_to_all(table, ('member', 'grid'), split_axis=0, concat_axis=0, ti...  7.06 us
    pallas_call x1, Pallas kernels, assemble(): pl.pallas_call(assemble_kernel, grid=(groups,), out_shape=jax.ShapeDtypeS...  4.56 us
    all_to_all x1, starting transfers between devices, on_device(): lax.all_to_all(result, 'member', split_axis=0, concat_axis=0, tiled=True)  4.13 us
  transfers between devices with their start and end apart: 5, of which 2 were waited for; matrix products, arithmetic and copies ran while one was open for 9% of the time, Pallas kernels for 30%

commit v1 on v0

v1 whole, which is shorter than its diff:
```python
import functools

import jax
import jax.numpy as jnp
from jax import lax
from jax.experimental import pallas as pl
from jax.experimental.pallas import tpu as pltpu
from jax.sharding import PartitionSpec as P

RIM = 16
LANES = 128
MESH = pl.DeviceIdType.MESH


def member_peer(me, r, n):
    if n & (n - 1):
        return lax.rem(me + r, n)
    peer = me
    bit = 1
    while bit < n:
        if r & bit:
            peer = peer + bit * (1 - 2 * lax.rem(me // bit, 2))
        bit *= 2
    return peer


def exchange_kernel(
    groups,
    patches,
    mapping_hbm,
    triples_hbm,
    factors_hbm,
    transforms_hbm,
    prior_hbm,
    out_hbm,
    mapping_ref,
    triples_ref,
    factors_ref,
    t32_ref,
    tall_ref,
    meta_out_ref,
    meta_in_ref,
    meta_ref,
    ids_ref,
    share_ref,
    x_ref,
    dev_ref,
    mean_ref,
    spread_ref,
    w_ref,
    result_ref,
    local_sem,
    own_sem,
    xs_sem,
    xr_sem,
    ts_sem,
    tr_sem,
    fs_sem,
    fr_sem,
    ms_sem,
    mr_sem,
    ns_sem,
    nr_sem,
    os_sem,
    or_sem,
    keep_sem,
):
    me = lax.axis_index("member")
    region = lax.axis_index("grid")
    chunks, _, mine, fields, width = x_ref.shape
    members = mine * groups
    columns = chunks * width
    pairs, coarse = tall_ref.shape
    coarse_dev = coarse // patches
    per_source = mapping_ref.shape[2]
    blocks = columns // LANES
    partner = region + 1 - 2 * lax.rem(region, 2)

    barrier = pltpu.get_barrier_semaphore()
    for r in range(1, groups):
        pl.semaphore_signal(
            barrier, inc=1, device_id={"member": member_peer(me, r, groups)}, device_id_type=MESH
        )
    for d in range(1, patches):
        pl.semaphore_signal(
            barrier, inc=1, device_id={"grid": lax.rem(region + d, patches)}, device_id_type=MESH
        )
    pl.semaphore_wait(barrier, groups + patches - 2)

    def forecast(c, r):
        peer = member_peer(me, r, groups)
        at = pl.ds(pl.multiple_of(peer * columns + c * width, width), width)
        return pltpu.make_async_remote_copy(
            src_ref=prior_hbm.at[:, :, at],
            dst_ref=x_ref.at[c, me],
            send_sem=xs_sem.at[c, r],
            recv_sem=xr_sem.at[c, r],
            device_id={"member": peer},
            device_id_type=MESH,
        )

    def own_forecast(c):
        at = pl.ds(pl.multiple_of(me * columns + c * width, width), width)
        return pltpu.make_async_copy(prior_hbm.at[:, :, at], x_ref.at[c, me], own_sem.at[c])

    def send_forecasts(first, last):
        def some(c, carry):
            for r in range(1, groups):
                forecast(c, r).start()
            return carry

        lax.fori_loop(first, last, some, 0)

    early = (chunks + 1) // 2
    send_forecasts(0, early)

    local = [
        pltpu.make_async_copy(triples_hbm.at[0], triples_ref, local_sem.at[0]),
        pltpu.make_async_copy(factors_hbm.at[0], factors_ref, local_sem.at[1]),
        pltpu.make_async_copy(transforms_hbm, t32_ref, local_sem.at[2]),
        pltpu.make_async_copy(mapping_hbm, mapping_ref, local_sem.at[3]),
    ]
    for copy in local:
        copy.start()
    lax.fori_loop(0, chunks, lambda c, z: (own_forecast(c).start(), z)[1], 0)

    local[0].wait()
    local[1].wait()
    raw = factors_ref[...]
    shares = raw / jnp.sum(raw, axis=0, keepdims=True)
    points = triples_ref[...].astype(jnp.float32)
    here = jnp.zeros((1, per_source), jnp.float32) + region.astype(jnp.float32)
    blank = jnp.zeros((1, per_source), jnp.float32)
    if per_source < LANES:
        meta_out_ref[...] = jnp.zeros_like(meta_out_ref)
    for h in range(patches):
        part = slice(h * per_source, (h + 1) * per_source)
        meta_out_ref[h, :, 0:per_source] = jnp.concatenate(
            [points[:, part], shares[:, part], here, blank], axis=0
        )

    def table(d):
        peer = lax.rem(region + d, patches)
        return pltpu.make_async_remote_copy(
            src_ref=meta_out_ref.at[peer],
            dst_ref=meta_in_ref.at[region],
            send_sem=ms_sem.at[d],
            recv_sem=mr_sem.at[d],
            device_id={"grid": peer},
            device_id_type=MESH,
        )

    for d in range(1, patches):
        table(d).start()
    meta_in_ref[region] = meta_out_ref[region]

    local[2].wait()

    def block_of(q):
        return tall_ref.at[:, pl.ds(pl.multiple_of(q * coarse_dev, coarse_dev), coarse_dev)]

    rows = pairs // 10

    def narrow(i, carry):
        at = pl.ds(pl.multiple_of(i * rows, rows), rows)
        lanes = pl.ds(pl.multiple_of(region * coarse_dev, coarse_dev), coarse_dev)
        tall_ref[at, lanes] = t32_ref[at, :].astype(jnp.bfloat16)
        return carry

    lax.fori_loop(0, 10, narrow, 0)
    half = patches // 2

    def transforms_far(d):
        return pltpu.make_async_remote_copy(
            src_ref=block_of(region),
            dst_ref=block_of(region),
            send_sem=ts_sem.at[d],
            recv_sem=tr_sem.at[d],
            device_id={"grid": lax.rem(region + 2 * d, patches)},
            device_id_type=MESH,
        )

    def transforms_near(d):
        source = lax.rem(region - 2 * d + patches, patches)
        return pltpu.make_async_remote_copy(
            src_ref=block_of(source),
            dst_ref=block_of(source),
            send_sem=fs_sem.at[d],
            recv_sem=fr_sem.at[d],
            device_id={"grid": partner},
            device_id_type=MESH,
        )

    for d in range(1, half):
        transforms_far(d).start()
    transforms_near(0).start()

    for d in range(1, patches):
        table(d).wait_recv()
    for gp in range(half):
        meta_ref[me, gp] = meta_in_ref[2 * gp : 2 * gp + 2].reshape(16, LANES).astype(jnp.bfloat16)

    def tables(r):
        return pltpu.make_async_remote_copy(
            src_ref=meta_ref.at[me],
            dst_ref=meta_ref.at[me],
            send_sem=ns_sem.at[r],
            recv_sem=nr_sem.at[r],
            device_id={"member": member_peer(me, r, groups)},
            device_id_type=MESH,
        )

    for r in range(1, groups):
        tables(r).start()
    send_forecasts(early, chunks)

    def arrive(c):
        own_forecast(c).wait()
        for r in range(1, groups):
            forecast(c, r).wait_recv()

    def center(c):
        for lane in range(0, width, LANES):
            lanes = slice(lane, lane + LANES)

            def add(kk, total, lanes=lanes):
                for g in range(groups):
                    total = total + x_ref[c, g, kk, :, lanes].astype(jnp.float32)
                return total

            total = lax.fori_loop(0, mine, add, jnp.zeros((fields, LANES), jnp.float32))
            mean = total / members
            mean_ref[c, :, lanes] = mean

            def less(kk, carry, lanes=lanes, mean=mean):
                for g in range(groups):
                    d = x_ref[c, g, kk, :, lanes].astype(jnp.float32) - mean
                    dev_ref[c, g * mine + kk, :, lanes] = d.astype(jnp.bfloat16).astype(jnp.float32)
                return carry

            lax.fori_loop(0, mine, less, 0)

    def early_center(c, carry):
        arrive(c)
        center(c)
        return carry

    lax.fori_loop(0, early, early_center, 0)

    local[3].wait()
    for r in range(1, groups):
        tables(r).wait_recv()
    cells = lax.broadcasted_iota(jnp.int32, (columns, per_source), 0) + me * columns

    def look(gp, found):
        for m in range(groups):
            both = meta_ref[m, gp]
            if per_source < LANES:
                both = both[:, 0:per_source]
            for side in range(2):
                spots = mapping_ref[2 * gp + side, m : m + 1, :]
                onehot = jnp.where(cells == spots, 1.0, 0.0).astype(jnp.bfloat16)
                hit = lax.dot_general(
                    both, onehot, (((1,), (1,)), ((), ())), preferred_element_type=jnp.float32
                )
                found = found + hit[8 * side : 8 * side + 8]
        return found

    found = lax.fori_loop(0, half, look, jnp.zeros((8, columns), jnp.float32))
    ids = found[0:3] + (found[6:7] * coarse_dev - RIM)
    ids = jnp.where(ids < 0.0, ids + coarse, ids)
    ids = jnp.where(ids >= coarse, ids - coarse, ids)
    for c in range(chunks):
        ids_ref[c, 0:3] = ids[:, c * width : (c + 1) * width]
        share_ref[c, 0:3] = found[3:6, c * width : (c + 1) * width]

    lax.fori_loop(early, chunks - 1, early_center, 0)

    for d in range(1, half):
        transforms_far(d).wait_recv()
        transforms_near(d).start()
    for d in range(half):
        transforms_near(d).wait_recv()

    def result(b, r):
        peer = member_peer(me, r, groups)
        at = pl.ds(pl.multiple_of(me * columns + b * LANES, LANES), LANES)
        return pltpu.make_async_remote_copy(
            src_ref=result_ref.at[b, pl.ds(peer * mine, mine)],
            dst_ref=out_hbm.at[:, :, at],
            send_sem=os_sem.at[b, r],
            recv_sem=or_sem.at[b, r],
            device_id={"member": peer},
            device_id_type=MESH,
        )

    def own_result(b):
        at = pl.ds(pl.multiple_of(me * columns + b * LANES, LANES), LANES)
        return pltpu.make_async_copy(
            result_ref.at[b, pl.ds(me * mine, mine)], out_hbm.at[:, :, at], keep_sem.at[b]
        )

    step = pairs // 4
    unroll = 8

    def update(c, carry):
        @pl.when(c == chunks - 1)
        def _():
            arrive(c)
            center(c)

        def place(q, z):
            at = pl.multiple_of(q * coarse_dev, coarse_dev)
            slots = lax.broadcasted_iota(jnp.int32, (coarse_dev, width), 0) + at
            slots = slots.astype(jnp.float32)
            spread = jnp.zeros((coarse_dev, width), jnp.float32)
            for s in range(3):
                hit = ids_ref[c, s : s + 1, :] == slots
                spread = spread + jnp.where(hit, share_ref[c, s : s + 1, :], 0.0)
            spread_ref[pl.ds(at, coarse_dev), :] = spread.astype(jnp.bfloat16)
            return z

        lax.fori_loop(0, patches, place, 0)

        def blend(i, z):
            at = pl.ds(pl.multiple_of(i * step, step), step)
            part = jnp.dot(tall_ref[at, :], spread_ref[...], preferred_element_type=jnp.float32)
            w_ref[pl.ds(i * (step // 8), step // 8)] = part.reshape(step // 8, 8, width)
            return z

        lax.fori_loop(0, 4, blend, 0)

        for lane in range(0, width, LANES):
            lanes = slice(lane, lane + LANES)
            b = c * (width // LANES) + lane // LANES

            def contract(jg, z, lanes=lanes, b=b):
                for first in (0, 4):

                    def some(kk, accs, first=first):
                        accs = list(accs)
                        for u in range(unroll):
                            k = kk * unroll + u
                            d = dev_ref[c, k, :, lanes]
                            for jj in range(4):
                                row = first + jj
                                w = w_ref[k * (members // 8) + jg, row : row + 1, lanes]
                                accs[jj] = accs[jj] + d * w
                        return tuple(accs)

                    start = tuple(mean_ref[c, :, lanes] for _ in range(4))
                    accs = lax.fori_loop(0, members // unroll, some, start)
                    for jj in range(4):
                        result_ref[b, jg * 8 + first + jj] = accs[jj].astype(jnp.bfloat16)
                return z

            lax.fori_loop(0, members // 8, contract, 0)
            for r in range(1, groups):
                result(b, r).start()
            own_result(b).start()
        return carry

    lax.fori_loop(0, chunks, update, 0)

    for d in range(1, patches):
        table(d).wait_send()
    for r in range(1, groups):
        tables(r).wait_send()
    for d in range(1, half):
        transforms_far(d).wait_send()
    for d in range(half):
        transforms_near(d).wait_send()

    def sent(c, carry):
        for r in range(1, groups):
            forecast(c, r).wait_send()
        return carry

    lax.fori_loop(0, chunks, sent, 0)

    def finish(b, carry):
        own_result(b).wait()
        for r in range(1, groups):
            result(b, r).wait()
        return carry

    lax.fori_loop(0, blocks, finish, 0)


def on_device(prior, mapping, triples, factors, transforms):
    groups = lax.axis_size("member")
    patches = lax.axis_size("grid")
    mine, fields, cells = prior.shape
    members = mine * groups
    columns = cells // groups
    per_source = mapping.shape[2]
    pairs, coarse_dev = transforms.shape
    coarse = coarse_dev * patches
    width = min(256, columns)
    chunks = columns // width
    blocks = columns // LANES
    anywhere = pl.BlockSpec(memory_space=pl.ANY)
    dma = pltpu.SemaphoreType.DMA
    return pl.pallas_call(
        functools.partial(exchange_kernel, groups, patches),
        out_shape=jax.ShapeDtypeStruct(prior.shape, jnp.bfloat16),
        in_specs=[anywhere] * 5,
        out_specs=anywhere,
        scratch_shapes=[
            pltpu.VMEM((patches, groups, per_source), jnp.int32),
            pltpu.VMEM((3, columns), jnp.int32),
            pltpu.VMEM((3, columns), jnp.float32),
            pltpu.VMEM((pairs, coarse_dev), jnp.float32),
            pltpu.VMEM((pairs, coarse), jnp.bfloat16),
            pltpu.VMEM((patches, 8, LANES), jnp.float32),
            pltpu.VMEM((patches, 8, LANES), jnp.float32),
            pltpu.VMEM((groups, patches // 2, 16, LANES), jnp.bfloat16),
            pltpu.VMEM((chunks, 8, width), jnp.float32),
            pltpu.VMEM((chunks, 8, width), jnp.float32),
            pltpu.VMEM((chunks, groups, mine, fields, width), jnp.bfloat16),
            pltpu.VMEM((chunks, members, fields, width), jnp.float32),
            pltpu.VMEM((chunks, fields, width), jnp.float32),
            pltpu.VMEM((coarse, width), jnp.bfloat16),
            pltpu.VMEM((pairs // 8, 8, width), jnp.float32),
            pltpu.VMEM((blocks, members, fields, LANES), jnp.bfloat16),
            dma((4,)),
            dma((chunks,)),
            dma((chunks, groups)),
            dma((chunks, groups)),
            dma((patches // 2,)),
            dma((patches // 2,)),
            dma((patches // 2,)),
            dma((patches // 2,)),
            dma((patches,)),
            dma((patches,)),
            dma((groups,)),
            dma((groups,)),
            dma((blocks, groups)),
            dma((blocks, groups)),
            dma((blocks,)),
        ],
        compiler_params=pltpu.CompilerParams(
            collective_id=0, has_side_effects=True, vmem_limit_bytes=60 * 1024 * 1024
        ),
        name="exchange",
    )(mapping, triples, factors, transforms, prior)


def solution(mesh):
    return jax.shard_map(
        on_device,
        mesh=mesh,
        in_specs=(
            P("member", None, "grid"),
            P(None, None, "grid"),
            P("grid", None, "member"),
            P("grid", None, "member"),
            P(None, "grid"),
        ),
        out_specs=P("member", None, "grid"),
        check_vma=False,
    )
```

time: 163 us -> 103 us (0.63)
  Pallas kernels: 52.4 us -> 95.6 us
  waiting for transfers between devices: 29 us -> 0 us
  blocking collectives: 28.5 us -> 0 us
  starting transfers between devices: 18.7 us -> 0 us
  between operations: 13.5 us -> 0.01 us
  other arithmetic: 8.24 us -> 0 us
  matrix products: 2.61 us -> 0 us
  local copies, waits for them, and re-layouts: 8.79 us -> 7.11 us
    pallas_call x3 -> x1, Pallas kernels: 52.4 us -> 95.6 us  [on_device(): pl.pallas_call(functools.partial(exchange_kernel, groups, patches), out_s...]
    all_to_all x4 -> x0, waiting for transfers between devices: 29 us -> none  [the longest x2 22 us: on_device(): lax.all_to_all(blocks, 'member', split_axis=0, concat_axis=0, tiled=True)]
    all_to_all x1 -> x0, blocking collectives: 28.5 us -> none  [on_device(): lax.all_to_all(result, 'member', split_axis=0, concat_axis=0, tiled=True)]
    all_to_all x4 -> x0, starting transfers between devices: 18.6 us -> none  [the longest x1 7.33 us: on_device(): lax.all_to_all(table, ('member', 'grid'), split_axis=0, concat_axis=0, ti...]
    another operation x2 -> x0, other arithmetic: 4.1 us -> none  [on_device(): blocks = jnp.stack([prior[:, :, at:at + part] for at in starts])]
    unnamed x15 -> x3, local copies, waits for them, and re-layouts: 3.31 us -> 7.11 us
    another operation x1 -> x0, local copies, waits for them, and re-layouts: 3.57 us -> none  [on_device(): blocks = jnp.stack([prior[:, :, at:at + part] for at in starts])]
    convert_element_type x4 -> x0, other arithmetic: 2.68 us -> none  [the longest x1 1.93 us: on_device(): transforms.astype(jnp.bfloat16)]
  transfers between devices with their start and end apart: 5 -> 0, of which waited for: 2 -> 0; matrix products, arithmetic and copies ran while one was open for 9% -> 0% of each run, Pallas kernels for 30% -> 0%
where the time goes in v1:
time: 103 us
  Pallas kernels  95.6 us (93%)
  local copies, waits for them, and re-layouts  7.11 us (7%)
    pallas_call x1, Pallas kernels, on_device(): pl.pallas_call(functools.partial(exchange_kernel, groups, patches), out_s...  95.6 us
    unnamed x3, local copies, waits for them, and re-layouts  7.11 us

profile of v1, /device:TPU:0, one launch (start us, length us, event | category | flops | bytes accessed | tf_op | source)
XLA Modules:
  0.0 102.7 jit_solution(6685097087077143800)
XLA Ops:
  0.0 1.3 %copy.6.triples_hbm = s32[1,3,1024]{2,1,0:T(4,128)} copy(s32[1,3,1024]{2,0,1:T(1,128)} %param.7) | data formatting | bytes 24576 | tf_op args[2]
  1.3 1.3 %copy.7.factors_hbm = f32[1,3,1024]{2,1,0:T(4,128)} copy(f32[1,3,1024]{2,0,1:T(1,128)} %param.8) | data formatting | bytes 24576 | tf_op args[3]
  2.6 95.6 %exchange.1 = bf16[10,48,4096]{2,1,0:T(8,128)(2,1)} custom-call(s32[8,4,128]{2,1,0:T(4,128)} %mapping_hbm.1, s32[1,3,1024]{2,1,0:T(4,128)} %copy.6.triples_hbm, f32[1,3,1024]{2,1,0:T(4,128)} %copy.7.factors_hbm, f32[1600,128]{1,0:T(8,128)} %transforms_hbm.1, bf16[10,48,4096]{2,1,0:T(8,128)(2,1)} %prior_hbm.1), custom_call_target="tpu_custom_call" | custom-call | tf_op jit(solution)/shard_map/exchange/pallas_call | solution.py:404
  98.2 4.5 %copy.9 = bf16[10,48,4096]{2,1,0:T(8,128)(2,1)} copy(bf16[10,48,4096]{2,1,0:T(8,128)(2,1)} %exchange.1) | data formatting | bytes 7864320

commit v2 on v1

--- a/solution.py
+++ b/solution.py
@@ -63,7 +63,6 @@
     nr_sem,
     os_sem,
     or_sem,
-    keep_sem,
 ):
     me = lax.axis_index("member")
     region = lax.axis_index("grid")
@@ -115,8 +114,8 @@
     send_forecasts(0, early)
 
     local = [
-        pltpu.make_async_copy(triples_hbm.at[0], triples_ref, local_sem.at[0]),
-        pltpu.make_async_copy(factors_hbm.at[0], factors_ref, local_sem.at[1]),
+        pltpu.make_async_copy(triples_hbm.at[:, 0], triples_ref, local_sem.at[0]),
+        pltpu.make_async_copy(factors_hbm.at[:, 0], factors_ref, local_sem.at[1]),
         pltpu.make_async_copy(transforms_hbm, t32_ref, local_sem.at[2]),
         pltpu.make_async_copy(mapping_hbm, mapping_ref, local_sem.at[3]),
     ]
@@ -296,9 +295,12 @@
 
     def own_result(b):
         at = pl.ds(pl.multiple_of(me * columns + b * LANES, LANES), LANES)
-        return pltpu.make_async_copy(
-            result_ref.at[b, pl.ds(me * mine, mine)], out_hbm.at[:, :, at], keep_sem.at[b]
-        )
+
+        def put(kk, carry):
+            out_hbm[kk, :, at] = result_ref[b, me * mine + kk]
+            return carry
+
+        lax.fori_loop(0, mine, put, 0)
 
     step = pairs // 4
     unroll = 8
@@ -357,7 +359,7 @@
             lax.fori_loop(0, members // 8, contract, 0)
             for r in range(1, groups):
                 result(b, r).start()
-            own_result(b).start()
+            own_result(b)
         return carry
 
     lax.fori_loop(0, chunks, update, 0)
@@ -379,7 +381,6 @@
     lax.fori_loop(0, chunks, sent, 0)
 
     def finish(b, carry):
-        own_result(b).wait()
         for r in range(1, groups):
             result(b, r).wait()
         return carry
@@ -403,9 +404,9 @@
     dma = pltpu.SemaphoreType.DMA
     return pl.pallas_call(
         functools.partial(exchange_kernel, groups, patches),
-        out_shape=jax.ShapeDtypeStruct(prior.shape, jnp.bfloat16),
+        out_shape=pltpu.VMEM(prior.shape, jnp.bfloat16),
         in_specs=[anywhere] * 5,
-        out_specs=anywhere,
+        out_specs=pl.BlockSpec(memory_space=pltpu.VMEM),
         scratch_shapes=[
             pltpu.VMEM((patches, groups, per_source), jnp.int32),
             pltpu.VMEM((3, columns), jnp.int32),
@@ -437,13 +438,21 @@
             dma((groups,)),
             dma((blocks, groups)),
             dma((blocks, groups)),
-            dma((blocks,)),
         ],
         compiler_params=pltpu.CompilerParams(
-            collective_id=0, has_side_effects=True, vmem_limit_bytes=60 * 1024 * 1024
+            collective_id=0, has_side_effects=True, vmem_limit_bytes=44 * 1024 * 1024
         ),
         name="exchange",
-    )(mapping, triples, factors, transforms, prior)
+    )(*[
+        pltpu.with_memory_space_constraint(a, pltpu.HBM)
+        for a in (
+            mapping,
+            jnp.transpose(triples, (1, 0, 2)),
+            jnp.transpose(factors, (1, 0, 2)),
+            transforms,
+            prior,
+        )
+    ])
 
 
 def solution(mesh):

time: 103 us -> 97.5 us (0.947)
  local copies, waits for them, and re-layouts: 7.11 us -> 1.93 us
    unnamed x3 -> x1, local copies, waits for them, and re-layouts: 7.11 us -> 1.93 us
where the time goes in v2:
time: 97.5 us; the launch traced here: 97.3 us
  Pallas kernels  95.4 us (98%)
  local copies, waits for them, and re-layouts  1.93 us (2%)
    pallas_call x1, Pallas kernels, on_device(): pl.pallas_call(functools.partial(exchange_kernel, groups, patches), out_s...  95.4 us

profile of v2, /device:TPU:0, one launch (start us, length us, event | category | flops | bytes accessed | tf_op | source)
XLA Modules:
  0.0 97.3 jit_solution(18138247293281638396)
XLA Ops:
  0.0 95.4 %exchange.1 = bf16[10,48,4096]{2,1,0:T(8,128)(2,1)S(1)} custom-call(s32[8,4,128]{2,1,0:T(4,128)} %mapping_hbm.1, s32[3,1,1024]{2,1,0:T(1,128)} %bitcast.2, f32[3,1,1024]{2,1,0:T(1,128)} %bitcast.3, f32[1600,128]{1,0:T(8,128)} %transforms_hbm.1, bf16[10,48,4096]{2,1,0:T(8,128)(2,1)} %prior_hbm.1), custom_call_target="tpu_custom_call" | custom-call | tf_op jit(solution)/shard_map/exchange/pallas_call | solution.py:405
  95.4 1.9 %copy.7 = bf16[10,48,4096]{2,1,0:T(8,128)(2,1)} copy(bf16[10,48,4096]{2,1,0:T(8,128)(2,1)S(1)} %exchange.1) | data formatting | bytes 7864320

commit v3 on v2

--- a/solution.py
+++ b/solution.py
@@ -53,6 +53,8 @@
     own_sem,
     xs_sem,
     xr_sem,
+    near_sem,
+    far_sem,
     ts_sem,
     tr_sem,
     fs_sem,
@@ -75,16 +77,41 @@
     blocks = columns // LANES
     partner = region + 1 - 2 * lax.rem(region, 2)
 
+    core = lax.rem(region, 2)
+    spot = region // 2
+    spots = patches // 2
     barrier = pltpu.get_barrier_semaphore()
-    for r in range(1, groups):
-        pl.semaphore_signal(
-            barrier, inc=1, device_id={"member": member_peer(me, r, groups)}, device_id_type=MESH
-        )
-    for d in range(1, patches):
-        pl.semaphore_signal(
-            barrier, inc=1, device_id={"grid": lax.rem(region + d, patches)}, device_id_type=MESH
-        )
-    pl.semaphore_wait(barrier, groups + patches - 2)
+    for r in range(groups):
+        hub = {"member": member_peer(me, r, groups), "grid": 2 * spot + 1}
+        if r:
+            pl.semaphore_signal(barrier, inc=1, device_id=hub, device_id_type=MESH)
+        else:
+
+            @pl.when(core == 0)
+            def _(hub=hub):
+                pl.semaphore_signal(barrier, inc=1, device_id=hub, device_id_type=MESH)
+
+    @pl.when(core == 1)
+    def _():
+        pl.semaphore_wait(barrier, 2 * groups - 1)
+        pl.semaphore_signal(near_sem, inc=1, device_id={"grid": partner}, device_id_type=MESH)
+
+    @pl.when(core == 0)
+    def _():
+        pl.semaphore_wait(near_sem, 1)
+        for d in range(1, spots):
+            other = 2 * lax.rem(spot + d, spots)
+            pl.semaphore_signal(barrier, inc=1, device_id={"grid": other}, device_id_type=MESH)
+
+    def meet_grid():
+        @pl.when(core == 0)
+        def _():
+            pl.semaphore_wait(barrier, spots - 1)
+            pl.semaphore_signal(far_sem, inc=1, device_id={"grid": partner}, device_id_type=MESH)
+
+        @pl.when(core == 1)
+        def _():
+            pl.semaphore_wait(far_sem, 1)
 
     def forecast(c, r):
         peer = member_peer(me, r, groups)
@@ -149,10 +176,6 @@
             device_id_type=MESH,
         )
 
-    for d in range(1, patches):
-        table(d).start()
-    meta_in_ref[region] = meta_out_ref[region]
-
     local[2].wait()
 
     def block_of(q):
@@ -167,36 +190,63 @@
         return carry
 
     lax.fori_loop(0, 10, narrow, 0)
-    half = patches // 2
-
-    def transforms_far(d):
+    def along(way, s):
+        block = block_of(region - 2 * way * s)
         return pltpu.make_async_remote_copy(
-            src_ref=block_of(region),
-            dst_ref=block_of(region),
-            send_sem=ts_sem.at[d],
-            recv_sem=tr_sem.at[d],
-            device_id={"grid": lax.rem(region + 2 * d, patches)},
+            src_ref=block,
+            dst_ref=block,
+            send_sem=ts_sem.at[(1 + way) // 2, s],
+            recv_sem=tr_sem.at[(1 + way) // 2, s],
+            device_id={"grid": region + 2 * way},
             device_id_type=MESH,
         )
 
-    def transforms_near(d):
-        source = lax.rem(region - 2 * d + patches, patches)
+    def across(at):
+        block = block_of(2 * at + core)
         return pltpu.make_async_remote_copy(
-            src_ref=block_of(source),
-            dst_ref=block_of(source),
-            send_sem=fs_sem.at[d],
-            recv_sem=fr_sem.at[d],
+            src_ref=block,
+            dst_ref=block,
+            send_sem=fs_sem.at[at],
+            recv_sem=fr_sem.at[at],
             device_id={"grid": partner},
             device_id_type=MESH,
         )
 
-    for d in range(1, half):
-        transforms_far(d).start()
-    transforms_near(0).start()
+    def has_next(way):
+        return spot + 1 < spots if way == 1 else spot > 0
+
+    def has_source(way, s):
+        return spot >= s if way == 1 else spot + s < spots
+
+    def relay(s):
+        for way in (1, -1):
+
+            @pl.when(has_source(way, s))
+            def _(way=way):
+                along(way, s - 1).wait_recv()
+
+                @pl.when(has_next(way))
+                def _():
+                    along(way, s).start()
+
+                across(spot - way * s).start()
+
+    meet_grid()
+    for d in range(1, patches):
+        table(d).start()
+    meta_in_ref[region] = meta_out_ref[region]
+
+    for way in (1, -1):
+
+        @pl.when(has_next(way))
+        def _(way=way):
+            along(way, 0).start()
+
+    across(spot).start()
 
     for d in range(1, patches):
         table(d).wait_recv()
-    for gp in range(half):
+    for gp in range(spots):
         meta_ref[me, gp] = meta_in_ref[2 * gp : 2 * gp + 2].reshape(16, LANES).astype(jnp.bfloat16)
 
     def tables(r):
@@ -244,7 +294,10 @@
         center(c)
         return carry
 
-    lax.fori_loop(0, early, early_center, 0)
+    early_center(0, 0)
+    for step_along in range(1, (spots + 1) // 2 + 1):
+        relay(step_along)
+    lax.fori_loop(1, early, early_center, 0)
 
     local[3].wait()
     for r in range(1, groups):
@@ -265,7 +318,7 @@
                 found = found + hit[8 * side : 8 * side + 8]
         return found
 
-    found = lax.fori_loop(0, half, look, jnp.zeros((8, columns), jnp.float32))
+    found = lax.fori_loop(0, spots, look, jnp.zeros((8, columns), jnp.float32))
     ids = found[0:3] + (found[6:7] * coarse_dev - RIM)
     ids = jnp.where(ids < 0.0, ids + coarse, ids)
     ids = jnp.where(ids >= coarse, ids - coarse, ids)
@@ -273,13 +326,10 @@
         ids_ref[c, 0:3] = ids[:, c * width : (c + 1) * width]
         share_ref[c, 0:3] = found[3:6, c * width : (c + 1) * width]
 
-    lax.fori_loop(early, chunks - 1, early_center, 0)
-
-    for d in range(1, half):
-        transforms_far(d).wait_recv()
-        transforms_near(d).start()
-    for d in range(half):
-        transforms_near(d).wait_recv()
+    for step_along in range((spots + 1) // 2 + 1, spots):
+        relay(step_along)
+    for at in range(spots):
+        across(at).wait_recv()
 
     def result(b, r):
         peer = member_peer(me, r, groups)
@@ -306,7 +356,7 @@
     unroll = 8
 
     def update(c, carry):
-        @pl.when(c == chunks - 1)
+        @pl.when(c >= early)
         def _():
             arrive(c)
             center(c)
@@ -368,10 +418,15 @@
         table(d).wait_send()
     for r in range(1, groups):
         tables(r).wait_send()
-    for d in range(1, half):
-        transforms_far(d).wait_send()
-    for d in range(half):
-        transforms_near(d).wait_send()
+    for s in range(spots - 1):
+        for way in (1, -1):
+
+            @pl.when(has_next(way) & has_source(way, s))
+            def _(way=way, s=s):
+                along(way, s).wait_send()
+
+    for at in range(spots):
+        across(at).wait_send()
 
     def sent(c, carry):
         for r in range(1, groups):
@@ -428,8 +483,10 @@
             dma((chunks,)),
             dma((chunks, groups)),
             dma((chunks, groups)),
-            dma((patches // 2,)),
-            dma((patches // 2,)),
+            pltpu.SemaphoreType.REGULAR,
+            pltpu.SemaphoreType.REGULAR,
+            dma((2, patches // 2)),
+            dma((2, patches // 2)),
             dma((patches // 2,)),
             dma((patches // 2,)),
             dma((patches,)),

time: 97.5 us -> 94.5 us (0.969)
  Pallas kernels: 95.4 us -> 92.4 us
    pallas_call x1, Pallas kernels: 95.4 us -> 92.4 us  [on_device(): pl.pallas_call(functools.partial(exchange_kernel, groups, patches), out_s...]
where the time goes in v3:
time: 94.5 us; the launch traced here: 94.4 us
  Pallas kernels  92.4 us (98%)
  local copies, waits for them, and re-layouts  1.93 us (2%)
    pallas_call x1, Pallas kernels, on_device(): pl.pallas_call(functools.partial(exchange_kernel, groups, patches), out_s...  92.4 us
    unnamed x1, local copies, waits for them, and re-layouts  1.93 us

profile of v3, /device:TPU:0, one launch (start us, length us, event | category | flops | bytes accessed | tf_op | source)
XLA Modules:
  0.0 94.4 jit_solution(14746977612868076084)
XLA Ops:
  0.0 92.4 %exchange.1 = bf16[10,48,4096]{2,1,0:T(8,128)(2,1)S(1)} custom-call(s32[8,4,128]{2,1,0:T(4,128)} %mapping_hbm.1, s32[3,1,1024]{2,1,0:T(1,128)} %bitcast.2, f32[3,1,1024]{2,1,0:T(1,128)} %bitcast.3, f32[1600,128]{1,0:T(8,128)} %transforms_hbm.1, bf16[10,48,4096]{2,1,0:T(8,128)(2,1)} %prior_hbm.1), custom_call_target="tpu_custom_call" | custom-call | tf_op jit(solution)/shard_map/exchange/pallas_call | solution.py:460
  92.4 1.9 %copy.7 = bf16[10,48,4096]{2,1,0:T(8,128)(2,1)} copy(bf16[10,48,4096]{2,1,0:T(8,128)(2,1)S(1)} %exchange.1) | data formatting | bytes 7864320

commit v4 on v3

--- a/solution.py
+++ b/solution.py
@@ -49,8 +49,9 @@
     spread_ref,
     w_ref,
     result_ref,
+    stage_ref,
     local_sem,
-    own_sem,
+    stage_sem,
     xs_sem,
     xr_sem,
     near_sem,
@@ -74,7 +75,6 @@
     pairs, coarse = tall_ref.shape
     coarse_dev = coarse // patches
     per_source = mapping_ref.shape[2]
-    blocks = columns // LANES
     partner = region + 1 - 2 * lax.rem(region, 2)
 
     core = lax.rem(region, 2)
@@ -91,18 +91,6 @@
             def _(hub=hub):
                 pl.semaphore_signal(barrier, inc=1, device_id=hub, device_id_type=MESH)
 
-    @pl.when(core == 1)
-    def _():
-        pl.semaphore_wait(barrier, 2 * groups - 1)
-        pl.semaphore_signal(near_sem, inc=1, device_id={"grid": partner}, device_id_type=MESH)
-
-    @pl.when(core == 0)
-    def _():
-        pl.semaphore_wait(near_sem, 1)
-        for d in range(1, spots):
-            other = 2 * lax.rem(spot + d, spots)
-            pl.semaphore_signal(barrier, inc=1, device_id={"grid": other}, device_id_type=MESH)
-
     def meet_grid():
         @pl.when(core == 0)
         def _():
@@ -113,21 +101,17 @@
         def _():
             pl.semaphore_wait(far_sem, 1)
 
-    def forecast(c, r):
+    def forecast(c, r, staged=False):
         peer = member_peer(me, r, groups)
         at = pl.ds(pl.multiple_of(peer * columns + c * width, width), width)
         return pltpu.make_async_remote_copy(
-            src_ref=prior_hbm.at[:, :, at],
+            src_ref=stage_ref.at[r - 1] if staged else prior_hbm.at[:, :, at],
             dst_ref=x_ref.at[c, me],
-            send_sem=xs_sem.at[c, r],
-            recv_sem=xr_sem.at[c, r],
+            send_sem=xs_sem,
+            recv_sem=xr_sem.at[c],
             device_id={"member": peer},
             device_id_type=MESH,
         )
-
-    def own_forecast(c):
-        at = pl.ds(pl.multiple_of(me * columns + c * width, width), width)
-        return pltpu.make_async_copy(prior_hbm.at[:, :, at], x_ref.at[c, me], own_sem.at[c])
 
     def send_forecasts(first, last):
         def some(c, carry):
@@ -137,9 +121,13 @@
 
         lax.fori_loop(first, last, some, 0)
 
+    def arrived(ref, sem):
+        pltpu.make_async_copy(ref, ref, sem).wait()
+
     early = (chunks + 1) // 2
-    send_forecasts(0, early)
-
+    for r in range(1, groups):
+        at = pl.ds(pl.multiple_of(member_peer(me, r, groups) * columns, width), width)
+        pltpu.make_async_copy(prior_hbm.at[:, :, at], stage_ref.at[r - 1], stage_sem).start()
     local = [
         pltpu.make_async_copy(triples_hbm.at[:, 0], triples_ref, local_sem.at[0]),
         pltpu.make_async_copy(factors_hbm.at[:, 0], factors_ref, local_sem.at[1]),
@@ -148,7 +136,30 @@
     ]
     for copy in local:
         copy.start()
-    lax.fori_loop(0, chunks, lambda c, z: (own_forecast(c).start(), z)[1], 0)
+    arrived(stage_ref, stage_sem)
+
+    @pl.when(core == 1)
+    def _():
+        pl.semaphore_wait(barrier, 2 * groups - 1)
+        pl.semaphore_signal(near_sem, inc=1, device_id={"grid": partner}, device_id_type=MESH)
+
+    @pl.when(core == 0)
+    def _():
+        pl.semaphore_wait(near_sem, 1)
+        for d in range(1, spots):
+            other = 2 * lax.rem(spot + d, spots)
+            pl.semaphore_signal(barrier, inc=1, device_id={"grid": other}, device_id_type=MESH)
+
+    for r in range(1, groups):
+        forecast(0, r, True).start()
+    send_forecasts(1, early)
+
+    def own_forecast(c, carry):
+        at = pl.ds(pl.multiple_of(me * columns + c * width, width), width)
+        pltpu.make_async_copy(prior_hbm.at[:, :, at], x_ref.at[c, me], xr_sem.at[c]).start()
+        return carry
+
+    lax.fori_loop(0, chunks, own_forecast, 0)
 
     local[0].wait()
     local[1].wait()
@@ -170,8 +181,8 @@
         return pltpu.make_async_remote_copy(
             src_ref=meta_out_ref.at[peer],
             dst_ref=meta_in_ref.at[region],
-            send_sem=ms_sem.at[d],
-            recv_sem=mr_sem.at[d],
+            send_sem=ms_sem,
+            recv_sem=mr_sem,
             device_id={"grid": peer},
             device_id_type=MESH,
         )
@@ -206,8 +217,8 @@
         return pltpu.make_async_remote_copy(
             src_ref=block,
             dst_ref=block,
-            send_sem=fs_sem.at[at],
-            recv_sem=fr_sem.at[at],
+            send_sem=fs_sem,
+            recv_sem=fr_sem,
             device_id={"grid": partner},
             device_id_type=MESH,
         )
@@ -244,8 +255,7 @@
 
     across(spot).start()
 
-    for d in range(1, patches):
-        table(d).wait_recv()
+    arrived(meta_in_ref.at[1:], mr_sem)
     for gp in range(spots):
         meta_ref[me, gp] = meta_in_ref[2 * gp : 2 * gp + 2].reshape(16, LANES).astype(jnp.bfloat16)
 
@@ -253,8 +263,8 @@
         return pltpu.make_async_remote_copy(
             src_ref=meta_ref.at[me],
             dst_ref=meta_ref.at[me],
-            send_sem=ns_sem.at[r],
-            recv_sem=nr_sem.at[r],
+            send_sem=ns_sem,
+            recv_sem=nr_sem,
             device_id={"member": member_peer(me, r, groups)},
             device_id_type=MESH,
         )
@@ -264,9 +274,7 @@
     send_forecasts(early, chunks)
 
     def arrive(c):
-        own_forecast(c).wait()
-        for r in range(1, groups):
-            forecast(c, r).wait_recv()
+        arrived(x_ref.at[c], xr_sem.at[c])
 
     def center(c):
         for lane in range(0, width, LANES):
@@ -300,8 +308,7 @@
     lax.fori_loop(1, early, early_center, 0)
 
     local[3].wait()
-    for r in range(1, groups):
-        tables(r).wait_recv()
+    arrived(meta_ref.at[1:], nr_sem)
     cells = lax.broadcasted_iota(jnp.int32, (columns, per_source), 0) + me * columns
 
     def look(gp, found):
@@ -328,8 +335,7 @@
 
     for step_along in range((spots + 1) // 2 + 1, spots):
         relay(step_along)
-    for at in range(spots):
-        across(at).wait_recv()
+    arrived(tall_ref.at[:, 0 : spots * coarse_dev], fr_sem)
 
     def result(b, r):
         peer = member_peer(me, r, groups)
@@ -337,8 +343,8 @@
         return pltpu.make_async_remote_copy(
             src_ref=result_ref.at[b, pl.ds(peer * mine, mine)],
             dst_ref=out_hbm.at[:, :, at],
-            send_sem=os_sem.at[b, r],
-            recv_sem=or_sem.at[b, r],
+            send_sem=os_sem,
+            recv_sem=or_sem,
             device_id={"member": peer},
             device_id_type=MESH,
         )
@@ -414,10 +420,8 @@
 
     lax.fori_loop(0, chunks, update, 0)
 
-    for d in range(1, patches):
-        table(d).wait_send()
-    for r in range(1, groups):
-        tables(r).wait_send()
+    arrived(meta_in_ref.at[1:], ms_sem)
+    arrived(meta_ref.at[1:], ns_sem)
     for s in range(spots - 1):
         for way in (1, -1):
 
@@ -425,22 +429,11 @@
             def _(way=way, s=s):
                 along(way, s).wait_send()
 
-    for at in range(spots):
-        across(at).wait_send()
-
-    def sent(c, carry):
-        for r in range(1, groups):
-            forecast(c, r).wait_send()
-        return carry
-
-    lax.fori_loop(0, chunks, sent, 0)
-
-    def finish(b, carry):
-        for r in range(1, groups):
-            result(b, r).wait()
-        return carry
-
-    lax.fori_loop(0, blocks, finish, 0)
+    arrived(tall_ref.at[:, 0 : spots * coarse_dev], fs_sem)
+    others = x_ref.at[:, 1:]
+    arrived(others, xs_sem)
+    arrived(others, os_sem)
+    arrived(others, or_sem)
 
 
 def on_device(prior, mapping, triples, factors, transforms):
@@ -479,22 +472,23 @@
             pltpu.VMEM((coarse, width), jnp.bfloat16),
             pltpu.VMEM((pairs // 8, 8, width), jnp.float32),
             pltpu.VMEM((blocks, members, fields, LANES), jnp.bfloat16),
+            pltpu.VMEM((groups - 1, mine, fields, width), jnp.bfloat16),
             dma((4,)),
+            dma,
+            dma,
             dma((chunks,)),
-            dma((chunks, groups)),
-            dma((chunks, groups)),
             pltpu.SemaphoreType.REGULAR,
             pltpu.SemaphoreType.REGULAR,
             dma((2, patches // 2)),
             dma((2, patches // 2)),
-            dma((patches // 2,)),
-            dma((patches // 2,)),
-            dma((patches,)),
-            dma((patches,)),
-            dma((groups,)),
-            dma((groups,)),
-            dma((blocks, groups)),
-            dma((blocks, groups)),
+            dma,
+            dma,
+            dma,
+            dma,
+            dma,
+            dma,
+            dma,
+            dma,
         ],
         compiler_params=pltpu.CompilerParams(
             collective_id=0, has_side_effects=True, vmem_limit_bytes=44 * 1024 * 1024

time: 94.5 us -> 93.3 us (0.987)
  Pallas kernels: 92.4 us -> 91.2 us
    pallas_call x1, Pallas kernels: 92.4 us -> 91.2 us  [on_device(): pl.pallas_call(functools.partial(exchange_kernel, groups, patches), out_s...]
where the time goes in v4:
time: 93.3 us; the launch traced here: 93.1 us
  Pallas kernels  91.2 us (98%)
  local copies, waits for them, and re-layouts  1.93 us (2%)
    pallas_call x1, Pallas kernels, on_device(): pl.pallas_call(functools.partial(exchange_kernel, groups, patches), out_s...  91.2 us
    unnamed x1, local copies, waits for them, and re-layouts  1.93 us

profile of v4, /device:TPU:0, one launch (start us, length us, event | category | flops | bytes accessed | tf_op | source)
XLA Modules:
  0.0 93.1 jit_solution(15687761808110574102)
XLA Ops:
  0.0 91.2 %exchange.1 = bf16[10,48,4096]{2,1,0:T(8,128)(2,1)S(1)} custom-call(s32[8,4,128]{2,1,0:T(4,128)} %mapping_hbm.1, s32[3,1,1024]{2,1,0:T(1,128)} %bitcast.2, f32[3,1,1024]{2,1,0:T(1,128)} %bitcast.3, f32[1600,128]{1,0:T(8,128)} %transforms_hbm.1, bf16[10,48,4096]{2,1,0:T(8,128)(2,1)} %prior_hbm.1), custom_call_target="tpu_custom_call" | custom-call | tf_op jit(solution)/shard_map/exchange/pallas_call | solution.py:453
  91.2 1.9 %copy.7 = bf16[10,48,4096]{2,1,0:T(8,128)(2,1)} copy(bf16[10,48,4096]{2,1,0:T(8,128)(2,1)S(1)} %exchange.1) | data formatting | bytes 7864320

commit v5 on v4

--- a/solution.py
+++ b/solution.py
@@ -9,6 +9,7 @@
 
 RIM = 16
 LANES = 128
+HALVES = 2
 MESH = pl.DeviceIdType.MESH
 
 
@@ -165,15 +166,14 @@
     local[1].wait()
     raw = factors_ref[...]
     shares = raw / jnp.sum(raw, axis=0, keepdims=True)
-    points = triples_ref[...].astype(jnp.float32)
-    here = jnp.zeros((1, per_source), jnp.float32) + region.astype(jnp.float32)
-    blank = jnp.zeros((1, per_source), jnp.float32)
+    points = triples_ref[...].astype(jnp.float32) + 1.0
+    blank = jnp.zeros((2, per_source), jnp.float32)
     if per_source < LANES:
         meta_out_ref[...] = jnp.zeros_like(meta_out_ref)
     for h in range(patches):
         part = slice(h * per_source, (h + 1) * per_source)
         meta_out_ref[h, :, 0:per_source] = jnp.concatenate(
-            [points[:, part], shares[:, part], here, blank], axis=0
+            [points[:, part], shares[:, part], blank], axis=0
         )
 
     def table(d):
@@ -189,8 +189,10 @@
 
     local[2].wait()
 
-    def block_of(q):
-        return tall_ref.at[:, pl.ds(pl.multiple_of(q * coarse_dev, coarse_dev), coarse_dev)]
+    def block_of(q, part):
+        rows = pairs // HALVES
+        lanes = pl.ds(pl.multiple_of(q * coarse_dev, coarse_dev), coarse_dev)
+        return tall_ref.at[part * rows : (part + 1) * rows, lanes]
 
     rows = pairs // 10
 
@@ -201,19 +203,19 @@
         return carry
 
     lax.fori_loop(0, 10, narrow, 0)
-    def along(way, s):
-        block = block_of(region - 2 * way * s)
+    def along(way, s, part):
+        block = block_of(region - 2 * way * s, part)
         return pltpu.make_async_remote_copy(
             src_ref=block,
             dst_ref=block,
-            send_sem=ts_sem.at[(1 + way) // 2, s],
-            recv_sem=tr_sem.at[(1 + way) // 2, s],
+            send_sem=ts_sem.at[(1 + way) // 2],
+            recv_sem=tr_sem.at[(1 + way) // 2, s, part],
             device_id={"grid": region + 2 * way},
             device_id_type=MESH,
         )
 
-    def across(at):
-        block = block_of(2 * at + core)
+    def across(at, part):
+        block = block_of(2 * at + core, part)
         return pltpu.make_async_remote_copy(
             src_ref=block,
             dst_ref=block,
@@ -229,18 +231,18 @@
     def has_source(way, s):
         return spot >= s if way == 1 else spot + s < spots
 
-    def relay(s):
+    def relay(s, part):
         for way in (1, -1):
 
             @pl.when(has_source(way, s))
             def _(way=way):
-                along(way, s - 1).wait_recv()
+                along(way, s - 1, part).wait_recv()
 
                 @pl.when(has_next(way))
                 def _():
-                    along(way, s).start()
-
-                across(spot - way * s).start()
+                    along(way, s, part).start()
+
+                across(spot - way * s, part).start()
 
     meet_grid()
     for d in range(1, patches):
@@ -251,13 +253,16 @@
 
         @pl.when(has_next(way))
         def _(way=way):
-            along(way, 0).start()
-
-    across(spot).start()
+            for part in range(HALVES):
+                along(way, 0, part).start()
+
+    for part in range(HALVES):
+        across(spot, part).start()
 
     arrived(meta_in_ref.at[1:], mr_sem)
-    for gp in range(spots):
-        meta_ref[me, gp] = meta_in_ref[2 * gp : 2 * gp + 2].reshape(16, LANES).astype(jnp.bfloat16)
+    for first in range(0, patches, 8):
+        packed = jnp.concatenate([meta_in_ref[first + u, 0:6] for u in range(8)], axis=0)
+        meta_ref[me, first // 8] = packed.astype(jnp.bfloat16)
 
     def tables(r):
         return pltpu.make_async_remote_copy(
@@ -302,39 +307,49 @@
         center(c)
         return carry
 
+    hops = [(s, part) for s in range(1, spots) for part in range(HALVES)]
+    middle = HALVES * ((spots + 1) // 2)
+    for hop in hops[:1]:
+        relay(*hop)
     early_center(0, 0)
-    for step_along in range(1, (spots + 1) // 2 + 1):
-        relay(step_along)
+    for hop in hops[1:middle]:
+        relay(*hop)
     lax.fori_loop(1, early, early_center, 0)
 
     local[3].wait()
     arrived(meta_ref.at[1:], nr_sem)
     cells = lax.broadcasted_iota(jnp.int32, (columns, per_source), 0) + me * columns
 
-    def look(gp, found):
+    def look(octet, found):
+        ids, shares = found
         for m in range(groups):
-            both = meta_ref[m, gp]
+            packed = meta_ref[m, octet]
             if per_source < LANES:
-                both = both[:, 0:per_source]
-            for side in range(2):
-                spots = mapping_ref[2 * gp + side, m : m + 1, :]
-                onehot = jnp.where(cells == spots, 1.0, 0.0).astype(jnp.bfloat16)
+                packed = packed[:, 0:per_source]
+            for u in range(8):
+                source = 8 * octet + u
+                onehot = jnp.where(cells == mapping_ref[source, m : m + 1, :], 1.0, 0.0)
                 hit = lax.dot_general(
-                    both, onehot, (((1,), (1,)), ((), ())), preferred_element_type=jnp.float32
-                )
-                found = found + hit[8 * side : 8 * side + 8]
-        return found
-
-    found = lax.fori_loop(0, spots, look, jnp.zeros((8, columns), jnp.float32))
-    ids = found[0:3] + (found[6:7] * coarse_dev - RIM)
+                    packed,
+                    onehot.astype(jnp.bfloat16),
+                    (((1,), (1,)), ((), ())),
+                    preferred_element_type=jnp.float32,
+                )[6 * u : 6 * u + 6]
+                base = (jnp.int32(source * coarse_dev) - (RIM + 1)).astype(jnp.float32)
+                ids = ids + jnp.where(hit[0:1] > 0.5, hit[0:3] + base, 0.0)
+                shares = shares + hit[3:6]
+        return ids, shares
+
+    nothing = jnp.zeros((3, columns), jnp.float32)
+    ids, shares = lax.fori_loop(0, patches // 8, look, (nothing, nothing))
     ids = jnp.where(ids < 0.0, ids + coarse, ids)
     ids = jnp.where(ids >= coarse, ids - coarse, ids)
     for c in range(chunks):
         ids_ref[c, 0:3] = ids[:, c * width : (c + 1) * width]
-        share_ref[c, 0:3] = found[3:6, c * width : (c + 1) * width]
-
-    for step_along in range((spots + 1) // 2 + 1, spots):
-        relay(step_along)
+        share_ref[c, 0:3] = shares[:, c * width : (c + 1) * width]
+
+    for hop in hops[middle:]:
+        relay(*hop)
     arrived(tall_ref.at[:, 0 : spots * coarse_dev], fr_sem)
 
     def result(b, r):
@@ -422,12 +437,12 @@
 
     arrived(meta_in_ref.at[1:], ms_sem)
     arrived(meta_ref.at[1:], ns_sem)
-    for s in range(spots - 1):
-        for way in (1, -1):
-
-            @pl.when(has_next(way) & has_source(way, s))
-            def _(way=way, s=s):
-                along(way, s).wait_send()
+    for n in range(1, spots):
+        for side, mark in ((1, n - 1), (0, spots - n)):
+
+            @pl.when(spot == mark)
+            def _(n=n, side=side):
+                arrived(tall_ref.at[:, 0 : n * coarse_dev], ts_sem.at[side])
 
     arrived(tall_ref.at[:, 0 : spots * coarse_dev], fs_sem)
     others = x_ref.at[:, 1:]
@@ -463,7 +478,7 @@
             pltpu.VMEM((pairs, coarse), jnp.bfloat16),
             pltpu.VMEM((patches, 8, LANES), jnp.float32),
             pltpu.VMEM((patches, 8, LANES), jnp.float32),
-            pltpu.VMEM((groups, patches // 2, 16, LANES), jnp.bfloat16),
+            pltpu.VMEM((groups, patches // 8, 48, LANES), jnp.bfloat16),
             pltpu.VMEM((chunks, 8, width), jnp.float32),
             pltpu.VMEM((chunks, 8, width), jnp.float32),
             pltpu.VMEM((chunks, groups, mine, fields, width), jnp.bfloat16),
@@ -479,8 +494,8 @@
             dma((chunks,)),
             pltpu.SemaphoreType.REGULAR,
             pltpu.SemaphoreType.REGULAR,
-            dma((2, patches // 2)),
-            dma((2, patches // 2)),
+            dma((2,)),
+            dma((2, patches // 2 - 1, HALVES)),
             dma,
             dma,
             dma,

time: 93.3 us -> 93.1 us (level)
  no operation moved by 1% of the time
where the time goes in v5:
time: 93.1 us; the launch traced here: 93 us
  Pallas kernels  91.1 us (98%)
  local copies, waits for them, and re-layouts  1.93 us (2%)
    pallas_call x1, Pallas kernels, on_device(): pl.pallas_call(functools.partial(exchange_kernel, groups, patches), out_s...  91.1 us
    unnamed x1, local copies, waits for them, and re-layouts  1.93 us

profile of v5, /device:TPU:0, one launch (start us, length us, event | category | flops | bytes accessed | tf_op | source)
XLA Modules:
  0.0 93.0 jit_solution(15921417593378501025)
XLA Ops:
  0.0 91.1 %exchange.1 = bf16[10,48,4096]{2,1,0:T(8,128)(2,1)S(1)} custom-call(s32[8,4,128]{2,1,0:T(4,128)} %mapping_hbm.1, s32[3,1,1024]{2,1,0:T(1,128)} %bitcast.2, f32[3,1,1024]{2,1,0:T(1,128)} %bitcast.3, f32[1600,128]{1,0:T(8,128)} %transforms_hbm.1, bf16[10,48,4096]{2,1,0:T(8,128)(2,1)} %prior_hbm.1), custom_call_target="tpu_custom_call" | custom-call | tf_op jit(solution)/shard_map/exchange/pallas_call | solution.py:468
  91.1 1.9 %copy.7 = bf16[10,48,4096]{2,1,0:T(8,128)(2,1)} copy(bf16[10,48,4096]{2,1,0:T(8,128)(2,1)S(1)} %exchange.1) | data formatting | bytes 7864320

commit v6 on v5

--- a/solution.py
+++ b/solution.py
@@ -102,12 +102,18 @@
         def _():
             pl.semaphore_wait(far_sem, 1)
 
-    def forecast(c, r, staged=False):
+    def forecast(c, r, staged=0):
         peer = member_peer(me, r, groups)
         at = pl.ds(pl.multiple_of(peer * columns + c * width, width), width)
+        if staged == 1:
+            at = pl.ds(pl.multiple_of(peer * columns + LANES, LANES), width - LANES)
+        source = stage_ref.at[r - 1] if staged == 2 else prior_hbm.at[:, :, at]
+        target = x_ref.at[c, me]
+        if staged:
+            target = target.at[:, :, LANES:] if staged == 1 else target.at[:, :, 0:LANES]
         return pltpu.make_async_remote_copy(
-            src_ref=stage_ref.at[r - 1] if staged else prior_hbm.at[:, :, at],
-            dst_ref=x_ref.at[c, me],
+            src_ref=source,
+            dst_ref=target,
             send_sem=xs_sem,
             recv_sem=xr_sem.at[c],
             device_id={"member": peer},
@@ -127,7 +133,7 @@
 
     early = (chunks + 1) // 2
     for r in range(1, groups):
-        at = pl.ds(pl.multiple_of(member_peer(me, r, groups) * columns, width), width)
+        at = pl.ds(pl.multiple_of(member_peer(me, r, groups) * columns, LANES), LANES)
         pltpu.make_async_copy(prior_hbm.at[:, :, at], stage_ref.at[r - 1], stage_sem).start()
     local = [
         pltpu.make_async_copy(triples_hbm.at[:, 0], triples_ref, local_sem.at[0]),
@@ -151,8 +157,9 @@
             other = 2 * lax.rem(spot + d, spots)
             pl.semaphore_signal(barrier, inc=1, device_id={"grid": other}, device_id_type=MESH)
 
-    for r in range(1, groups):
-        forecast(0, r, True).start()
+    for staged in (2, 1):
+        for r in range(1, groups):
+            forecast(0, r, staged).start()
     send_forecasts(1, early)
 
     def own_forecast(c, carry):
@@ -487,7 +494,7 @@
             pltpu.VMEM((coarse, width), jnp.bfloat16),
             pltpu.VMEM((pairs // 8, 8, width), jnp.float32),
             pltpu.VMEM((blocks, members, fields, LANES), jnp.bfloat16),
-            pltpu.VMEM((groups - 1, mine, fields, width), jnp.bfloat16),
+            pltpu.VMEM((groups - 1, mine, fields, LANES), jnp.bfloat16),
             dma((4,)),
             dma,
             dma,

time: 93.1 us -> 92.9 us (level)
  no operation moved by 1% of the time
where the time goes in v6:
time: 92.9 us; the launch traced here: 92.8 us
  Pallas kernels  90.9 us (98%)
  local copies, waits for them, and re-layouts  1.93 us (2%)
    pallas_call x1, Pallas kernels, on_device(): pl.pallas_call(functools.partial(exchange_kernel, groups, patches), out_s...  90.9 us
    unnamed x1, local copies, waits for them, and re-layouts  1.93 us

profile of v6, /device:TPU:0, one launch (start us, length us, event | category | flops | bytes accessed | tf_op | source)
XLA Modules:
  0.0 92.8 jit_solution(4827652012762072010)
XLA Ops:
  0.0 90.9 %exchange.1 = bf16[10,48,4096]{2,1,0:T(8,128)(2,1)S(1)} custom-call(s32[8,4,128]{2,1,0:T(4,128)} %mapping_hbm.1, s32[3,1,1024]{2,1,0:T(1,128)} %bitcast.2, f32[3,1,1024]{2,1,0:T(1,128)} %bitcast.3, f32[1600,128]{1,0:T(8,128)} %transforms_hbm.1, bf16[10,48,4096]{2,1,0:T(8,128)(2,1)} %prior_hbm.1), custom_call_target="tpu_custom_call" | custom-call | tf_op jit(solution)/shard_map/exchange/pallas_call | solution.py:475
  90.9 1.9 %copy.7 = bf16[10,48,4096]{2,1,0:T(8,128)(2,1)} copy(bf16[10,48,4096]{2,1,0:T(8,128)(2,1)S(1)} %exchange.1) | data formatting | bytes 7864320

commit v7 on v6

--- a/solution.py
+++ b/solution.py
@@ -23,6 +23,13 @@
             peer = peer + bit * (1 - 2 * lax.rem(me // bit, 2))
         bit *= 2
     return peer
+
+
+def split_peers(n):
+    others = range(1, n)
+    if n & (n - 1):
+        return list(others), []
+    return [r for r in others if not r & (r - 1)], [r for r in others if r & (r - 1)]
 
 
 def exchange_kernel(
@@ -56,7 +63,9 @@
     xs_sem,
     xr_sem,
     near_sem,
+    all_sem,
     far_sem,
+    hub_sem,
     ts_sem,
     tr_sem,
     fs_sem,
@@ -81,16 +90,49 @@
     core = lax.rem(region, 2)
     spot = region // 2
     spots = patches // 2
+    near, far = split_peers(groups)
+    rounds = hub_sem.shape[0]
     barrier = pltpu.get_barrier_semaphore()
-    for r in range(groups):
+    for r in near:
         hub = {"member": member_peer(me, r, groups), "grid": 2 * spot + 1}
-        if r:
-            pl.semaphore_signal(barrier, inc=1, device_id=hub, device_id_type=MESH)
-        else:
-
-            @pl.when(core == 0)
-            def _(hub=hub):
-                pl.semaphore_signal(barrier, inc=1, device_id=hub, device_id_type=MESH)
+        pl.semaphore_signal(barrier, inc=1, device_id=hub, device_id_type=MESH)
+
+    @pl.when(core == 0)
+    def _():
+        pl.semaphore_signal(barrier, inc=1, device_id={"grid": partner}, device_id_type=MESH)
+
+    def tell_hubs(t):
+        for r in near:
+            hub = {"member": member_peer(me, r, groups)}
+            pl.semaphore_signal(hub_sem.at[t], inc=1, device_id=hub, device_id_type=MESH)
+
+    def meet_near():
+        @pl.when(core == 1)
+        def _():
+            pl.semaphore_wait(barrier, 2 * len(near) + 1)
+            pl.semaphore_signal(near_sem, inc=1, device_id={"grid": partner}, device_id_type=MESH)
+            if far:
+                tell_hubs(0)
+
+        @pl.when(core == 0)
+        def _():
+            pl.semaphore_wait(near_sem, 1)
+            for d in range(1, spots):
+                other = 2 * lax.rem(spot + d, spots)
+                pl.semaphore_signal(barrier, inc=1, device_id={"grid": other}, device_id_type=MESH)
+
+    def meet_all():
+        @pl.when(core == 1)
+        def _():
+            for t in range(rounds):
+                pl.semaphore_wait(hub_sem.at[t], len(near))
+                if t + 1 < rounds:
+                    tell_hubs(t + 1)
+            pl.semaphore_signal(all_sem, inc=1, device_id={"grid": partner}, device_id_type=MESH)
+
+        @pl.when(core == 0)
+        def _():
+            pl.semaphore_wait(all_sem, 1)
 
     def meet_grid():
         @pl.when(core == 0)
@@ -143,22 +185,15 @@
     ]
     for copy in local:
         copy.start()
+    meet_near()
     arrived(stage_ref, stage_sem)
-
-    @pl.when(core == 1)
-    def _():
-        pl.semaphore_wait(barrier, 2 * groups - 1)
-        pl.semaphore_signal(near_sem, inc=1, device_id={"grid": partner}, device_id_type=MESH)
-
-    @pl.when(core == 0)
-    def _():
-        pl.semaphore_wait(near_sem, 1)
-        for d in range(1, spots):
-            other = 2 * lax.rem(spot + d, spots)
-            pl.semaphore_signal(barrier, inc=1, device_id={"grid": other}, device_id_type=MESH)
-
     for staged in (2, 1):
-        for r in range(1, groups):
+        for r in near:
+            forecast(0, r, staged).start()
+    if far:
+        meet_all()
+    for staged in (2, 1):
+        for r in far:
             forecast(0, r, staged).start()
     send_forecasts(1, early)
 
@@ -501,6 +536,8 @@
             dma((chunks,)),
             pltpu.SemaphoreType.REGULAR,
             pltpu.SemaphoreType.REGULAR,
+            pltpu.SemaphoreType.REGULAR,
+            pltpu.SemaphoreType.REGULAR((max(groups.bit_length() - 2, 1),)),
             dma((2,)),
             dma((2, patches // 2 - 1, HALVES)),
             dma,

time: 92.9 us -> 93 us (level)
  no operation moved by 1% of the time
where the time goes in v7:
time: 93 us; the launch traced here: 92.9 us
  Pallas kernels  91 us (98%)
  local copies, waits for them, and re-layouts  1.93 us (2%)
    pallas_call x1, Pallas kernels, on_device(): pl.pallas_call(functools.partial(exchange_kernel, groups, patches), out_s...  91 us
    unnamed x1, local copies, waits for them, and re-layouts  1.93 us

profile of v7, /device:TPU:0, one launch (start us, length us, event | category | flops | bytes accessed | tf_op | source)
XLA Modules:
  0.0 92.9 jit_solution(5424109188653344302)
XLA Ops:
  0.0 91.0 %exchange.1 = bf16[10,48,4096]{2,1,0:T(8,128)(2,1)S(1)} custom-call(s32[8,4,128]{2,1,0:T(4,128)} %mapping_hbm.1, s32[3,1,1024]{2,1,0:T(1,128)} %bitcast.2, f32[3,1,1024]{2,1,0:T(1,128)} %bitcast.3, f32[1600,128]{1,0:T(8,128)} %transforms_hbm.1, bf16[10,48,4096]{2,1,0:T(8,128)(2,1)} %prior_hbm.1), custom_call_target="tpu_custom_call" | custom-call | tf_op jit(solution)/shard_map/exchange/pallas_call | solution.py:510
  91.0 1.9 %copy.7 = bf16[10,48,4096]{2,1,0:T(8,128)(2,1)} copy(bf16[10,48,4096]{2,1,0:T(8,128)(2,1)S(1)} %exchange.1) | data formatting | bytes 7864320
